TPU v7x, 32 devices: a whole 2x2x4 slice. The times are simulated.
32 devices in a mesh: rep: 4 (over z), own: 8 (over y, x, core).
Axes of the slice: x: 2, y: 2, z: 4, core: 2. Of those that a mesh axis runs over, the one named last changes fastest.
Arguments:
- inputs: bfloat16 [8192, 8192], P(('rep', 'own')), may hold values from -6 to 6
- cotangent: bfloat16 [8192, 8192], P(('rep', 'own')), may hold values from -6 to 6
- gate: float32 [8192], P(('rep', 'own')), may hold values from 0.05 to 0.95
- down_weight: bfloat16 [8192, 256], P('rep'), may hold values from -0.0625 to 0.0625
- up_weight: bfloat16 [8192, 256], P('rep'), may hold values from -0.0625 to 0.0625
- mixing: bfloat16 [256, 256], replicated, may hold values from -0.375 to 0.375
- owner_table: int32 [8, 8], replicated, may hold values from -1 to 31, as said below
- left_factor: float32 [64, 256, 256], P('own'), as said below
- right_factor: float32 [64, 256, 256], P('own'), as said below
Outputs:
- preconditioned: float32 [16384, 256], P('own')
Inputs may be any that keep to these rules, and one draw needn't show every extreme that they name: `owner_table`: each of the 32 block ids stands in exactly one slot; -1 marks an empty slot; some owner has all 8 slots filled. `left_factor`: every slot's matrix is symmetric positive definite. `right_factor`: every slot's matrix is symmetric positive definite.
All inputs are finite; a program needn't handle non-finite values.
Results may differ from a plain program's by a relative error of at most 0.0077.
Values may be sent and summed in bfloat16 or wider, within the bound.
No kernel may reach another device: no remote copies, remote signals or barrier semaphores. Data moves between devices by JAX's collectives and lax.ppermute only.
A program may use at most 128 MiB of HBM per device.

v0:
```python
import jax
import jax.numpy as jnp
from jax import lax
from jax.sharding import PartitionSpec as P

R = 256
ITERS = 5
BETA = 0.95
EPS = 1e-06


def batched(left, right):
    return jnp.einsum("kij,kjl->kil", left, right, precision=lax.Precision.HIGHEST)


def inverse_root(matrices):
    width = matrices.shape[-1]
    identity = jnp.eye(width, dtype=jnp.float32)
    shifted = matrices + EPS * identity
    norm_size = jnp.sqrt(jnp.sum(shifted * shifted, axis=(1, 2)))
    result = jnp.broadcast_to(identity, shifted.shape) * (norm_size ** (-0.25))[:, None, None]
    normed = shifted / norm_size[:, None, None]
    for sweep in range(ITERS):
        factor = (5.0 * identity - normed) / 4.0
        result = batched(result, factor)
        square = batched(factor, factor)
        normed = batched(batched(square, square), normed)
    return result


def shards(
    inputs, cotangent, gate, down_weight, up_weight, mixing, owner_table, left_factor, right_factor
):
    token_total = inputs.shape[0] * lax.axis_size("rep") * lax.axis_size("own")
    slot_count = left_factor.shape[0]
    lifted = (gate[:, None] * inputs.astype(jnp.float32) * cotangent.astype(jnp.float32)).astype(
        jnp.bfloat16
    )
    columns = inputs
    projected = jnp.dot(
        columns,
        lax.all_gather(down_weight, "rep", axis=0, tiled=True),
        preferred_element_type=jnp.float32,
    )
    back_proj = jnp.dot(
        lifted,
        lax.all_gather(up_weight, "rep", axis=0, tiled=True),
        preferred_element_type=jnp.float32,
    )
    inner_act = jnp.tanh(projected).astype(jnp.bfloat16)
    outer_act = jnp.tanh(jnp.dot(inner_act, mixing, preferred_element_type=jnp.float32))
    outer_slope = (back_proj * (1.0 - outer_act * outer_act)).astype(jnp.bfloat16)
    through = lax.dot_general(
        outer_slope, mixing, (((1,), (1,)), ((), ())), preferred_element_type=jnp.float32
    )
    inner_wide = inner_act.astype(jnp.float32)
    signal = (through * (1.0 - inner_wide * inner_wide)).astype(jnp.bfloat16)
    columns = inputs
    shard = lax.psum_scatter(
        lax.dot_general(
            columns, signal, (((0,), (0,)), ((), ())), preferred_element_type=jnp.float32
        )
        / token_total,
        "own",
        scatter_dimension=0,
        tiled=True,
    )
    shard = lax.psum(shard, "rep")
    my_blocks = lax.dynamic_index_in_dim(owner_table, lax.axis_index("own"), 0, keepdims=False)
    wanted = (
        jnp.maximum(my_blocks, 0)[:, None] * R + jnp.arange(R, dtype=jnp.int32)[None, :]
    ).reshape(-1)
    shard_rows = lax.all_gather(shard, "own", axis=0, tiled=True)
    row_total = shard_rows.shape[0]
    inside = (wanted >= 0) & (wanted < row_total)
    selected = jnp.take(shard_rows, jnp.clip(wanted, 0, row_total - 1), axis=0)
    owned = jnp.where(inside[:, None], selected, jnp.zeros((slot_count * R, R), jnp.float32))
    my_row = lax.dynamic_index_in_dim(owner_table, lax.axis_index("own"), 0, keepdims=False)
    filled_slots = (my_row >= 0)[:, None, None]
    gradients = jnp.where(filled_slots, owned.reshape(slot_count, R, R), 0.0)
    flipped = jnp.swapaxes(gradients, 1, 2)
    left_new = BETA * left_factor + (1.0 - BETA) * batched(gradients, flipped)
    right_new = BETA * right_factor + (1.0 - BETA) * batched(flipped, gradients)
    factors = jnp.concatenate([left_new, right_new], axis=0)
    inverse_roots = inverse_root(factors)
    preconditioned = batched(
        batched(inverse_roots[:slot_count], gradients), inverse_roots[slot_count:]
    )
    return jnp.where(filled_slots, preconditioned, 0.0).reshape(slot_count * R, R)


def solution(mesh):
    in_specs = (
        P(("rep", "own"), None),
        P(("rep", "own"), None),
        P(("rep", "own")),
        P("rep", None),
        P("rep", None),
        P(),
        P(),
        P("own", None, None),
        P("own", None, None),
    )
    out_specs = P("own", None)
    return jax.shard_map(shards, mesh=mesh, in_specs=in_specs, out_specs=out_specs, check_vma=False)
```

profile of v0, /device:TPU:0, one launch (start us, length us, event | category | flops | bytes accessed | tf_op | source)
XLA Modules:
  0.0 500.8 jit_solution(6470604852635249459)
XLA Ops:
  6.5 0.0 copy-start
  6.5 0.0 all-gather.6.cloned.1.call-start
  6.5 0.7 all-gather.6.cloned.1.call-update
  7.3 0.0 all-gather.4.cloned.1.call-start
  7.3 0.7 all-gather.4.cloned.1.call-update
  8.0 0.0 copy-start.3
  8.0 0.0 reduce-scatter.2.cloned.1.call-start
  8.1 84.3 %all-gather.6.cloned.1.call-done = bf16[8192,256]{1,0:T(8,128)(2,1)} async-done(((bf16[2048,256]{1,0:T(8,128)(2,1)}), bf16[8192,256]{1,0:T(8,128)(2,1)}) %all-gather.6.cloned.1.call-update) | async-done | bytes 4194320 | tf_op jit(solution)/shard_map/all_gather | solution.py:42
  92.4 4.7 fusion.47
  97.1 76.1 %all-gather.4.cloned.1.call-done = bf16[8192,256]{1,0:T(8,128)(2,1)} async-done(((bf16[2048,256]{1,0:T(8,128)(2,1)}), bf16[8192,256]{1,0:T(8,128)(2,1)}) %all-gather.4.cloned.1.call-update) | async-done | bytes 4194320 | tf_op jit(solution)/shard_map/all_gather | solution.py:47
  173.2 0.0 copy-done.3
  173.2 6.1 %fusion.1 = f32[256,256]{1,0:T(8,128)S(1)} fusion(bf16[8192,256]{1,0:T(8,128)(2,1)} %all-gather.4.cloned.1.call-done, bf16[256,8192]{1,0:T(8,128)(2,1)} %param.10, bf16[256,8192]{1,0:T(8,128)(2,1)} %param.9, f32[256]{0:T(256)S(1)} %copy-done.3), kind=kOutput, calls=%fused_computation.4 | convolution fusion | flops 1084227584 | bytes 12846080 | tf_op jit(solution)/shard_map/dot_general | solution.py:45
  179.3 0.0 copy-done
  179.4 0.3 fusion.46
  179.7 6.7 %fusion = f32[8192,256]{0,1:T(8,128)} fusion(bf16[256,256]{1,0:T(8,128)(2,1)S(1)} %fusion.46, bf16[256,8192]{1,0:T(8,128)(2,1)} %param.9), kind=kOutput, calls=%fused_computation.2 | convolution fusion | flops 1075838976 | bytes 12713984 | tf_op jit(solution)/shard_map/dot_general | solution.py:60
  186.4 0.0 reduce-scatter.2.cloned.1.call-update
  186.4 0.0 all-reduce.2.cloned.1.call-start
  186.5 70.0 %reduce-scatter.2.cloned.1.call-done = f32[1024,256]{0,1:T(8,128)} async-done(((f32[8192,256]{0,1:T(8,128)}), f32[1024,256]{0,1:T(8,128)}) %reduce-scatter.2.cloned.1.call-update) | async-done | bytes 1048592 | tf_op jit(solution)/shard_map/reduce_scatter | solution.py:59
  256.5 0.0 all-reduce.2.cloned.1.call-update
  256.5 0.0 all-gather.8.cloned.1.call-start
  256.5 54.1 %all-reduce.2.cloned.1.call-done = f32[1024,256]{0,1:T(8,128)} async-done(((f32[1024,256]{0,1:T(8,128)}), f32[1024,256]{0,1:T(8,128)}) %all-reduce.2.cloned.1.call-update) | async-done | bytes 1048592 | tf_op jit(solution)/shard_map/psum | solution.py:68
  310.6 0.0 all-gather.8.cloned.1.call-update
  310.6 0.7 multiply_bitcast_fusion
  311.3 0.1 fusion.70
  311.4 0.7 compare_bitcast_fusion
  312.2 0.1 fusion.74
  312.3 53.6 %all-gather.8.cloned.1.call-done = f32[8192,256]{0,1:T(8,128)} async-done(((f32[1024,256]{0,1:T(8,128)}), f32[8192,256]{0,1:T(8,128)}) %all-gather.8.cloned.1.call-update) | async-done | bytes 8388624 | tf_op jit(solution)/shard_map/all_gather | solution.py:73
  365.9 9.0 %copy.10 = f32[8192,256]{1,0:T(8,128)} copy(f32[8192,256]{0,1:T(8,128)} %all-gather.8.cloned.1.call-done) | data formatting | bytes 16777216 | tf_op jit(solution)/shard_map/all_gather | solution.py:73
  374.9 10.0 %gather_fusion = f32[2048,256]{1,0:T(8,128)S(1)} fusion(f32[8192,256]{1,0:T(8,128)} %copy.10, s32[2048]{0:T(1024)S(1)} %broadcast_clamp_fusion), kind=kCustom, calls=%fused_computation | custom fusion | bytes 4202496 | tf_op jit(solution)/shard_map/jit(_take)/gather | solution.py:76
  384.9 0.0 copy-start.2
  384.9 6.5 %multiply_add_fusion = f32[8,256,256]{2,1,0:T(8,128)S(1)} fusion(f32[8,256,256]{2,1,0:T(8,128)} %param.17, f32[8,256,256]{2,1,0:T(8,128)S(1)} %bitcast.43, pred[8]{0:T(512)(128)(4,1)S(1)} %compare_bitcast_fusion, pred[8,256]{1,0:T(8,128)(4,1)S(1)} %get-tuple-element.8, pred[8,256]{1,0:T(8,128)(4,1)S(1)} %get-tuple-element.7), kind=kOutput, calls=%fused_computation.46 | convolution fusion | flops 1613758464 | bytes 6295560 | tf_op jit(solution)/shard_map/kij,kjl->kil/dot_general | solution.py:13
  391.4 0.0 copy-done.2
  391.4 4.4 multiply_add_fusion.1
  395.8 0.6 multiply_reduce_fusion
  396.5 6.1 %fusion.8 = f32[16,256,256]{2,1,0:T(8,128)S(1)} fusion(f32[256,256]{1,0:T(8,128)S(1)} %get-tuple-element.9, f32[8,256,256]{2,1,0:T(8,128)S(1)} %multiply_add_fusion, f32[8,256,256]{2,1,0:T(8,128)S(1)} %multiply_add_fusion.1, f32[16]{0:T(128)S(1)} %get-tuple-element.5, f32[256,256]{1,0:T(8,128)S(1)} %get-tuple-element.10), kind=kOutput, calls=%fused_computation.17 | convolution fusion | flops 3226468352 | bytes 8912960 | tf_op jit(solution)/shard_map/kij,kjl->kil/dot_general | solution.py:13
  402.6 5.1 %fusion.96 = f32[16,256,256]{2,1,0:T(8,128)S(1)} fusion(f32[16,256,256]{2,1,0:T(8,128)S(1)} %fusion.8), kind=kOutput, calls=%fused_computation.115 | convolution fusion | flops 3221225472 | bytes 8388608 | tf_op jit(solution)/shard_map/kij,kjl->kil/dot_general | solution.py:13
  407.7 5.4 %fusion.92 = f32[16,256,256]{2,1,0:T(8,128)S(1)} fusion(f32[16,256,256]{2,1,0:T(8,128)S(1)} %fusion.96, f32[8,256,256]{2,1,0:T(8,128)S(1)} %multiply_add_fusion, f32[8,256,256]{2,1,0:T(8,128)S(1)} %multiply_add_fusion.1, f32[16]{0:T(128)S(1)} %get-tuple-element.5, f32[256,256]{1,0:T(8,128)S(1)} %get-tuple-element.10), kind=kOutput, calls=%fused_computation.113 | convolution fusion | flops 3224371200 | bytes 12845120 | tf_op jit(solution)/shard_map/kij,kjl->kil/dot_general | solution.py:13
  413.1 5.7 %fusion.9 = f32[16,256,256]{2,1,0:T(8,128)S(1)} fusion(f32[16,256,256]{2,1,0:T(8,128)S(1)} %fusion.92, f32[256,256]{1,0:T(8,128)S(1)} %get-tuple-element.9), kind=kOutput, calls=%fused_computation.18 | convolution fusion | flops 3223322624 | bytes 8650752 | tf_op jit(solution)/shard_map/kij,kjl->kil/dot_general | solution.py:13
  418.8 6.0 %fusion.5 = f32[16,256,256]{2,1,0:T(8,128)S(1)} fusion(f32[256,256]{1,0:T(8,128)S(1)} %get-tuple-element.9, f32[16]{0:T(128)S(1)} %get-tuple-element.6, f32[256,256]{1,0:T(8,128)S(1)} %fusion.65, f32[8,256,256]{2,1,0:T(8,128)S(1)} %multiply_add_fusion, f32[8,256,256]{2,1,0:T(8,128)S(1)} %multiply_add_fusion.1, f32[16]{0:T(128)S(1)} %get-tuple-element.5, ...), kind=kOutput, calls=%fused_computation.13 | convolution fusion | flops 3227516928 | bytes 9175168 | tf_op jit(solution)/shard_map/kij,kjl->kil/dot_general | solution.py:13
  424.8 5.3 %fusion.10 = f32[16,256,256]{2,1,0:T(8,128)S(1)} fusion(f32[16,256,256]{2,1,0:T(8,128)S(1)} %fusion.5, f32[16,256,256]{2,1,0:T(8,128)S(1)} %fusion.92, f32[256,256]{1,0:T(8,128)S(1)} %get-tuple-element.9), kind=kOutput, calls=%fused_computation.19 | convolution fusion | flops 3223322624 | bytes 12845056 | tf_op jit(solution)/shard_map/kij,kjl->kil/dot_general | solution.py:13
  430.1 5.1 %fusion.97 = f32[16,256,256]{2,1,0:T(8,128)S(1)} fusion(f32[16,256,256]{2,1,0:T(8,128)S(1)} %fusion.9), kind=kOutput, calls=%fused_computation.116 | convolution fusion | flops 3221225472 | bytes 8388608 | tf_op jit(solution)/shard_map/kij,kjl->kil/dot_general | solution.py:13
  435.2 5.2 %fusion.98 = f32[16,256,256]{2,1,0:T(8,128)S(1)} fusion(f32[16,256,256]{2,1,0:T(8,128)S(1)} %fusion.97, f32[16,256,256]{2,1,0:T(8,128)S(1)} %fusion.92), kind=kOutput, calls=%fused_computation.117 | convolution fusion | flops 3221225472 | bytes 12582912 | tf_op jit(solution)/shard_map/kij,kjl->kil/dot_general | solution.py:13
  440.4 5.6 %fusion.11 = f32[16,256,256]{2,1,0:T(8,128)S(1)} fusion(f32[16,256,256]{2,1,0:T(8,128)S(1)} %fusion.98, f32[256,256]{1,0:T(8,128)S(1)} %get-tuple-element.9), kind=kOutput, calls=%fused_computation.20 | convolution fusion | flops 3223322624 | bytes 8650752 | tf_op jit(solution)/shard_map/kij,kjl->kil/dot_general | solution.py:13
  446.0 5.4 %fusion.12 = f32[16,256,256]{2,1,0:T(8,128)S(1)} fusion(f32[16,256,256]{2,1,0:T(8,128)S(1)} %fusion.10, f32[16,256,256]{2,1,0:T(8,128)S(1)} %fusion.98, f32[256,256]{1,0:T(8,128)S(1)} %get-tuple-element.9), kind=kOutput, calls=%fused_computation.21 | convolution fusion | flops 3223322624 | bytes 12845056 | tf_op jit(solution)/shard_map/kij,kjl->kil/dot_general | solution.py:13
  451.4 5.0 fusion.99
  456.4 5.0 %fusion.100 = f32[16,256,256]{2,1,0:T(8,128)S(1)} fusion(f32[16,256,256]{2,1,0:T(8,128)S(1)} %fusion.99, f32[16,256,256]{2,1,0:T(8,128)S(1)} %fusion.98), kind=kOutput, calls=%fused_computation.119 | convolution fusion | flops 3221225472 | bytes 12582912 | tf_op jit(solution)/shard_map/kij,kjl->kil/dot_general | solution.py:13
  461.4 6.0 %fusion.13 = f32[16,256,256]{2,1,0:T(8,128)S(1)} fusion(f32[16,256,256]{2,1,0:T(8,128)S(1)} %fusion.100, f32[256,256]{1,0:T(8,128)S(1)} %get-tuple-element.9), kind=kOutput, calls=%fused_computation.22 | convolution fusion | flops 3223322624 | bytes 8650752 | tf_op jit(solution)/shard_map/kij,kjl->kil/dot_general | solution.py:13
  467.4 5.1 %fusion.14 = f32[16,256,256]{2,1,0:T(8,128)S(1)} fusion(f32[16,256,256]{2,1,0:T(8,128)S(1)} %fusion.12, f32[16,256,256]{2,1,0:T(8,128)S(1)} %fusion.100, f32[256,256]{1,0:T(8,128)S(1)} %get-tuple-element.9), kind=kOutput, calls=%fused_computation.23 | convolution fusion | flops 3223322624 | bytes 12845056 | tf_op jit(solution)/shard_map/kij,kjl->kil/dot_general | solution.py:13
  472.5 5.1 %fusion.101 = f32[16,256,256]{2,1,0:T(8,128)S(1)} fusion(f32[16,256,256]{2,1,0:T(8,128)S(1)} %fusion.13), kind=kOutput, calls=%fused_computation.120 | convolution fusion | flops 3221225472 | bytes 8388608 | tf_op jit(solution)/shard_map/kij,kjl->kil/dot_general | solution.py:13
  477.6 5.0 %fusion.102 = f32[16,256,256]{2,1,0:T(8,128)S(1)} fusion(f32[16,256,256]{2,1,0:T(8,128)S(1)} %fusion.101, f32[16,256,256]{2,1,0:T(8,128)S(1)} %fusion.100), kind=kOutput, calls=%fused_computation.121 | convolution fusion | flops 3221225472 | bytes 12582912 | tf_op jit(solution)/shard_map/kij,kjl->kil/dot_general | solution.py:13
  482.7 5.1 %fusion.2 = f32[16,256,256]{2,1,0:T(8,128)S(1)} fusion(f32[16,256,256]{2,1,0:T(8,128)S(1)} %fusion.14, f32[16,256,256]{2,1,0:T(8,128)S(1)} %fusion.102, f32[256,256]{1,0:T(8,128)S(1)} %get-tuple-element.9), kind=kOutput, calls=%fused_computation.6 | convolution fusion | flops 3223322624 | bytes 12845056 | tf_op jit(solution)/shard_map/kij,kjl->kil/dot_general | solution.py:13
  487.8 0.0 copy-start.1
  487.8 2.8 fusion.41
  490.6 3.5 fusion.38
  494.1 0.0 copy-done.1
  (6 shorter events, 0.1 us)
Async XLA Ops:
  6.5 172.8 %copy-start = (bf16[256,256]{1,0:T(8,128)(2,1)S(1)}, bf16[256,256]{1,0:T(8,128)(2,1)}, u32[]{:S(2)}) copy-start(bf16[256,256]{1,0:T(8,128)(2,1)} %param.14) | copy-start | bytes 393220
  6.5 85.9 %all-gather.6.cloned.1.call-start = ((), (), s32[]{:S(2)}) async-start(), calls=%async_computation.2 | async-start | bytes 5242880 | tf_op jit(solution)/shard_map/all_gather | solution.py:42
  7.3 166.0 %all-gather.4.cloned.1.call-start = ((), (), s32[]{:S(2)}) async-start(), calls=%async_computation.1 | async-start | bytes 5242880 | tf_op jit(solution)/shard_map/all_gather | solution.py:47
  8.0 165.2 %copy-start.3 = (f32[256]{0:T(256)S(1)}, f32[256]{0:T(256)}, u32[]{:S(2)}) copy-start(f32[256]{0:T(256)} %param.11) | copy-start | bytes 3076
  8.0 248.4 %reduce-scatter.2.cloned.1.call-start = ((), (), s32[]{:S(2)}) async-start(), calls=%async_computation.3 | async-start | bytes 9437184 | tf_op jit(solution)/shard_map/reduce_scatter | solution.py:59
  186.4 124.1 %all-reduce.2.cloned.1.call-start = ((), (), s32[]{:S(2)}) async-start(), calls=%async_computation.4 | async-start | bytes 2097152 | tf_op jit(solution)/shard_map/psum | solution.py:68
  256.5 109.4 %all-gather.8.cloned.1.call-start = ((), (), s32[]{:S(2)}) async-start(), calls=%async_computation.5 | async-start | bytes 9437184 | tf_op jit(solution)/shard_map/all_gather | solution.py:73
  384.9 6.5 %copy-start.2 = (f32[8,256,256]{2,1,0:T(8,128)S(1)}, f32[8,256,256]{2,1,0:T(8,128)}, u32[]{:S(2)}) copy-start(f32[8,256,256]{2,1,0:T(8,128)} %param.16) | copy-start | bytes 6291460
  487.8 6.3 %copy-start.1 = (bf16[256,256]{1,0:T(8,128)(2,1)S(1)}, bf16[256,256]{1,0:T(8,128)(2,1)}, u32[]{:S(2)}) copy-start(bf16[256,256]{1,0:T(8,128)(2,1)} %param.14) | copy-start | bytes 393220
Sparse Core Ops, SparseCore 0:
  8.9 83.4 all-gather.5
  94.0 79.2 all-gather.3
  186.6 69.8 reduce-scatter.1
  258.7 51.8 all-reduce.1
  312.3 53.5 all-gather.7
where the time goes:
time: 507 us; the launch traced here: 501 us
  waiting for transfers between devices  340 us (67%)
  matrix products  126 us (25%)
  local copies, waits for them, and re-layouts  19 us (4%)
  between operations  13.6 us (3%)
    dot_general x21, matrix products, batched(): jnp.einsum('kij,kjl->kil', left, right, precision=lax.Precision.HIGHEST)  108 us
    all_gather x1, waiting for transfers between devices, shards(): lax.all_gather(down_weight, 'rep', axis=0, tiled=True)  84.3 us
    all_gather x1, waiting for transfers between devices, shards(): lax.all_gather(up_weight, 'rep', axis=0, tiled=True)  76.1 us
    reduce_scatter x1, waiting for transfers between devices, shards(): lax.psum_scatter(lax.dot_general(columns, signal, (((0,), (0,)), ((), ())...  70 us
    psum x1, waiting for transfers between devices, shards(): shard = lax.psum(shard, 'rep')  54.1 us
    all_gather x1, waiting for transfers between devices, shards(): shard_rows = lax.all_gather(shard, 'own', axis=0, tiled=True)  53.6 us
  transfers between devices with their start and end apart: 5, of which 5 were waited for; matrix products, arithmetic and copies ran while one was open for 1% of the time, Pallas kernels for 0%

commit v1 on v0

--- a/solution.py
+++ b/solution.py
@@ -65,7 +65,7 @@
         scatter_dimension=0,
         tiled=True,
     )
-    shard = lax.psum(shard, "rep")
+    shard = jnp.sum(lax.all_gather(shard, "rep"), axis=0)
     my_blocks = lax.dynamic_index_in_dim(owner_table, lax.axis_index("own"), 0, keepdims=False)
     wanted = (
         jnp.maximum(my_blocks, 0)[:, None] * R + jnp.arange(R, dtype=jnp.int32)[None, :]

time: 507 us -> 538 us (1.061)
  waiting for transfers between devices: 340 us -> 365 us
    all_gather x0 -> x1, waiting for transfers between devices: none -> 82.1 us  [shards(): shard = jnp.sum(lax.all_gather(shard, 'rep'), axis=0)]
    psum x1 -> x0, waiting for transfers between devices: 54.1 us -> none  [shards(): shard = lax.psum(shard, 'rep')]
where the time goes in v1:
time: 538 us; the launch traced here: 530 us
  waiting for transfers between devices  365 us (68%)
  matrix products  126 us (23%)
  local copies, waits for them, and re-layouts  17.4 us (3%)
  between operations  13.8 us (3%)
  other arithmetic  7.01 us (1%)
    dot_general x21, matrix products, batched(): jnp.einsum('kij,kjl->kil', left, right, precision=lax.Precision.HIGHEST)  108 us
    all_gather x1, waiting for transfers between devices, shards(): lax.all_gather(down_weight, 'rep', axis=0, tiled=True)  84.3 us
    all_gather x1, waiting for transfers between devices, shards(): shard = jnp.sum(lax.all_gather(shard, 'rep'), axis=0)  82.1 us
    all_gather x1, waiting for transfers between devices, shards(): lax.all_gather(up_weight, 'rep', axis=0, tiled=True)  76.1 us
    reduce_scatter x1, waiting for transfers between devices, shards(): lax.psum_scatter(lax.dot_general(columns, signal, (((0,), (0,)), ((), ())...  70 us
    all_gather x1, waiting for transfers between devices, shards(): shard_rows = lax.all_gather(shard, 'own', axis=0, tiled=True)  51.2 us
  transfers between devices with their start and end apart: 5, of which 5 were waited for; matrix products, arithmetic and copies ran while one was open for 1% of the time, Pallas kernels for 0%

profile of v1, /device:TPU:0, one launch (start us, length us, event | category | flops | bytes accessed | tf_op | source)
XLA Modules:
  0.0 529.9 jit_solution(10177599287284923515)
XLA Ops:
  6.5 0.0 copy-start
  6.5 0.0 all-gather.8.cloned.1.call-start
  6.5 0.7 all-gather.8.cloned.1.call-update
  7.3 0.0 all-gather.6.cloned.1.call-start
  7.3 0.7 all-gather.6.cloned.1.call-update
  8.0 0.0 copy-start.3
  8.0 0.0 reduce-scatter.2.cloned.1.call-start
  8.1 84.3 %all-gather.8.cloned.1.call-done = bf16[8192,256]{1,0:T(8,128)(2,1)} async-done(((bf16[2048,256]{1,0:T(8,128)(2,1)}), bf16[8192,256]{1,0:T(8,128)(2,1)}) %all-gather.8.cloned.1.call-update) | async-done | bytes 4194320 | tf_op jit(solution)/shard_map/all_gather | solution.py:42
  92.4 4.7 fusion.47
  97.1 76.1 %all-gather.6.cloned.1.call-done = bf16[8192,256]{1,0:T(8,128)(2,1)} async-done(((bf16[2048,256]{1,0:T(8,128)(2,1)}), bf16[8192,256]{1,0:T(8,128)(2,1)}) %all-gather.6.cloned.1.call-update) | async-done | bytes 4194320 | tf_op jit(solution)/shard_map/all_gather | solution.py:47
  173.2 0.0 copy-done.3
  173.2 6.1 %fusion.1 = f32[256,256]{1,0:T(8,128)S(1)} fusion(bf16[8192,256]{1,0:T(8,128)(2,1)} %all-gather.6.cloned.1.call-done, bf16[256,8192]{1,0:T(8,128)(2,1)} %param.10, bf16[256,8192]{1,0:T(8,128)(2,1)} %param.9, f32[256]{0:T(256)S(1)} %copy-done.3), kind=kOutput, calls=%fused_computation.4 | convolution fusion | flops 1084227584 | bytes 12846080 | tf_op jit(solution)/shard_map/dot_general | solution.py:45
  179.3 0.0 copy-done
  179.4 0.3 fusion.46
  179.7 6.7 %fusion = f32[8192,256]{0,1:T(8,128)} fusion(bf16[256,256]{1,0:T(8,128)(2,1)S(1)} %fusion.46, bf16[256,8192]{1,0:T(8,128)(2,1)} %param.9), kind=kOutput, calls=%fused_computation.2 | convolution fusion | flops 1075838976 | bytes 12713984 | tf_op jit(solution)/shard_map/dot_general | solution.py:60
  186.4 0.0 reduce-scatter.2.cloned.1.call-update
  186.4 0.0 all-gather.12.cloned.1.call-start
  186.5 70.0 %reduce-scatter.2.cloned.1.call-done = f32[1024,256]{0,1:T(8,128)} async-done(((f32[8192,256]{0,1:T(8,128)}), f32[1024,256]{0,1:T(8,128)}) %reduce-scatter.2.cloned.1.call-update) | async-done | bytes 1048592 | tf_op jit(solution)/shard_map/reduce_scatter | solution.py:59
  256.5 0.0 all-gather.12.cloned.1.call-update
  256.5 0.0 all-gather.10.cloned.1.call-start
  256.5 82.1 %all-gather.12.cloned.1.call-done = f32[4096,256]{0,1:T(8,128)} async-done(((f32[1024,256]{0,1:T(8,128)}), f32[4096,256]{0,1:T(8,128)}) %all-gather.12.cloned.1.call-update) | async-done | bytes 4194320 | tf_op jit(solution)/shard_map/all_gather | solution.py:68
  338.7 6.0 %reshape.112 = f32[4,1024,256]{1,0,2:T(4,128)} reshape(f32[4096,256]{0,1:T(8,128)} %all-gather.12.cloned.1.call-done) | data formatting | bytes 8388608 | tf_op jit(solution)/shard_map/all_gather | solution.py:68
  344.7 4.7 reduce_sum.18
  349.5 1.3 copy.11
  350.8 0.0 all-gather.10.cloned.1.call-update
  350.8 0.7 multiply_bitcast_fusion
  351.5 0.1 fusion.70
  351.6 0.7 compare_bitcast_fusion
  352.3 0.1 fusion.74
  352.5 51.2 %all-gather.10.cloned.1.call-done = f32[8192,256]{1,0:T(8,128)} async-done(((f32[1024,256]{1,0:T(8,128)}), f32[8192,256]{1,0:T(8,128)}) %all-gather.10.cloned.1.call-update) | async-done | bytes 8388624 | tf_op jit(solution)/shard_map/all_gather | solution.py:73
  403.7 10.0 %gather_fusion = f32[2048,256]{1,0:T(8,128)S(1)} fusion(f32[8192,256]{1,0:T(8,128)} %all-gather.10.cloned.1.call-done, s32[2048]{0:T(1024)S(1)} %broadcast_clamp_fusion), kind=kCustom, calls=%fused_computation | custom fusion | bytes 4202496 | tf_op jit(solution)/shard_map/jit(_take)/gather | solution.py:76
  413.7 0.0 copy-start.2
  413.7 6.5 %multiply_add_fusion = f32[8,256,256]{2,1,0:T(8,128)S(1)} fusion(f32[8,256,256]{2,1,0:T(8,128)} %param.17, f32[8,256,256]{2,1,0:T(8,128)S(1)} %bitcast.45, pred[8]{0:T(512)(128)(4,1)S(1)} %compare_bitcast_fusion, pred[8,256]{1,0:T(8,128)(4,1)S(1)} %get-tuple-element.8, pred[8,256]{1,0:T(8,128)(4,1)S(1)} %get-tuple-element.7), kind=kOutput, calls=%fused_computation.46 | convolution fusion | flops 1613758464 | bytes 6295560 | tf_op jit(solution)/shard_map/kij,kjl->kil/dot_general | solution.py:13
  420.2 0.0 copy-done.2
  420.2 4.4 multiply_add_fusion.1
  424.7 0.6 multiply_reduce_fusion
  425.3 6.1 %fusion.8 = f32[16,256,256]{2,1,0:T(8,128)S(1)} fusion(f32[256,256]{1,0:T(8,128)S(1)} %get-tuple-element.9, f32[8,256,256]{2,1,0:T(8,128)S(1)} %multiply_add_fusion, f32[8,256,256]{2,1,0:T(8,128)S(1)} %multiply_add_fusion.1, f32[16]{0:T(128)S(1)} %get-tuple-element.5, f32[256,256]{1,0:T(8,128)S(1)} %get-tuple-element.10), kind=kOutput, calls=%fused_computation.17 | convolution fusion | flops 3226468352 | bytes 8912960 | tf_op jit(solution)/shard_map/kij,kjl->kil/dot_general | solution.py:13
  431.4 5.1 fusion.96
  436.6 5.6 %fusion.92 = f32[16,256,256]{2,1,0:T(8,128)S(1)} fusion(f32[16,256,256]{2,1,0:T(8,128)S(1)} %fusion.96, f32[8,256,256]{2,1,0:T(8,128)S(1)} %multiply_add_fusion, f32[8,256,256]{2,1,0:T(8,128)S(1)} %multiply_add_fusion.1, f32[16]{0:T(128)S(1)} %get-tuple-element.5, f32[256,256]{1,0:T(8,128)S(1)} %get-tuple-element.10), kind=kOutput, calls=%fused_computation.113 | convolution fusion | flops 3224371200 | bytes 12845120 | tf_op jit(solution)/shard_map/kij,kjl->kil/dot_general | solution.py:13
  442.2 5.7 %fusion.9 = f32[16,256,256]{2,1,0:T(8,128)S(1)} fusion(f32[16,256,256]{2,1,0:T(8,128)S(1)} %fusion.92, f32[256,256]{1,0:T(8,128)S(1)} %get-tuple-element.9), kind=kOutput, calls=%fused_computation.18 | convolution fusion | flops 3223322624 | bytes 8650752 | tf_op jit(solution)/shard_map/kij,kjl->kil/dot_general | solution.py:13
  447.8 5.8 %fusion.5 = f32[16,256,256]{2,1,0:T(8,128)S(1)} fusion(f32[256,256]{1,0:T(8,128)S(1)} %get-tuple-element.9, f32[16]{0:T(128)S(1)} %get-tuple-element.6, f32[256,256]{1,0:T(8,128)S(1)} %fusion.65, f32[8,256,256]{2,1,0:T(8,128)S(1)} %multiply_add_fusion, f32[8,256,256]{2,1,0:T(8,128)S(1)} %multiply_add_fusion.1, f32[16]{0:T(128)S(1)} %get-tuple-element.5, ...), kind=kOutput, calls=%fused_computation.13 | convolution fusion | flops 3227516928 | bytes 9175168 | tf_op jit(solution)/shard_map/kij,kjl->kil/dot_general | solution.py:13
  453.6 5.3 fusion.10
  458.9 5.1 fusion.97
  464.0 5.3 fusion.98
  469.3 5.6 %fusion.11 = f32[16,256,256]{2,1,0:T(8,128)S(1)} fusion(f32[16,256,256]{2,1,0:T(8,128)S(1)} %fusion.98, f32[256,256]{1,0:T(8,128)S(1)} %get-tuple-element.9), kind=kOutput, calls=%fused_computation.20 | convolution fusion | flops 3223322624 | bytes 8650752 | tf_op jit(solution)/shard_map/kij,kjl->kil/dot_general | solution.py:13
  474.9 5.6 %fusion.12 = f32[16,256,256]{2,1,0:T(8,128)S(1)} fusion(f32[16,256,256]{2,1,0:T(8,128)S(1)} %fusion.10, f32[16,256,256]{2,1,0:T(8,128)S(1)} %fusion.98, f32[256,256]{1,0:T(8,128)S(1)} %get-tuple-element.9), kind=kOutput, calls=%fused_computation.21 | convolution fusion | flops 3223322624 | bytes 12845056 | tf_op jit(solution)/shard_map/kij,kjl->kil/dot_general | solution.py:13
  480.5 5.0 fusion.99
  485.4 5.0 fusion.100
  490.4 5.7 %fusion.13 = f32[16,256,256]{2,1,0:T(8,128)S(1)} fusion(f32[16,256,256]{2,1,0:T(8,128)S(1)} %fusion.100, f32[256,256]{1,0:T(8,128)S(1)} %get-tuple-element.9), kind=kOutput, calls=%fused_computation.22 | convolution fusion | flops 3223322624 | bytes 8650752 | tf_op jit(solution)/shard_map/kij,kjl->kil/dot_general | solution.py:13
  496.2 5.1 fusion.14
  501.3 5.2 fusion.101
  506.5 5.0 fusion.102
  511.5 5.1 fusion.2
  516.7 0.0 copy-start.1
  516.7 2.8 fusion.41
  519.5 3.5 fusion.38
  523.0 0.0 copy-done.1
  (6 shorter events, 0.1 us)
Async XLA Ops:
  6.5 172.8 %copy-start = (bf16[256,256]{1,0:T(8,128)(2,1)S(1)}, bf16[256,256]{1,0:T(8,128)(2,1)}, u32[]{:S(2)}) copy-start(bf16[256,256]{1,0:T(8,128)(2,1)} %param.14) | copy-start | bytes 393220
  6.5 85.9 %all-gather.8.cloned.1.call-start = ((), (), s32[]{:S(2)}) async-start(), calls=%async_computation.2 | async-start | bytes 5242880 | tf_op jit(solution)/shard_map/all_gather | solution.py:42
  7.3 166.0 %all-gather.6.cloned.1.call-start = ((), (), s32[]{:S(2)}) async-start(), calls=%async_computation.1 | async-start | bytes 5242880 | tf_op jit(solution)/shard_map/all_gather | solution.py:47
  8.0 165.2 %copy-start.3 = (f32[256]{0:T(256)S(1)}, f32[256]{0:T(256)}, u32[]{:S(2)}) copy-start(f32[256]{0:T(256)} %param.11) | copy-start | bytes 3076
  8.0 248.4 %reduce-scatter.2.cloned.1.call-start = ((), (), s32[]{:S(2)}) async-start(), calls=%async_computation.3 | async-start | bytes 9437184 | tf_op jit(solution)/shard_map/reduce_scatter | solution.py:59
  186.4 152.2 %all-gather.12.cloned.1.call-start = ((), (), s32[]{:S(2)}) async-start(), calls=%async_computation.5 | async-start | bytes 5242880 | tf_op jit(solution)/shard_map/all_gather | solution.py:68
  256.5 147.2 %all-gather.10.cloned.1.call-start = ((), (), s32[]{:S(2)}) async-start(), calls=%async_computation.4 | async-start | bytes 9437184 | tf_op jit(solution)/shard_map/all_gather | solution.py:73
  413.7 6.5 %copy-start.2 = (f32[8,256,256]{2,1,0:T(8,128)S(1)}, f32[8,256,256]{2,1,0:T(8,128)}, u32[]{:S(2)}) copy-start(f32[8,256,256]{2,1,0:T(8,128)} %param.16) | copy-start | bytes 6291460
  516.7 6.3 %copy-start.1 = (bf16[256,256]{1,0:T(8,128)(2,1)S(1)}, bf16[256,256]{1,0:T(8,128)(2,1)}, u32[]{:S(2)}) copy-start(bf16[256,256]{1,0:T(8,128)(2,1)} %param.14) | copy-start | bytes 393220
Sparse Core Ops, SparseCore 0:
  8.9 83.4 all-gather.7
  94.0 79.2 all-gather.5
  186.6 69.8 reduce-scatter.1
  257.9 80.7 all-gather.11
  350.9 52.7 all-gather.9
